TPU v7x, 32 devices: a whole 2x2x4 slice. The times are simulated.
32 devices in a mesh: grp: 4 (over x, core), dev: 8 (over z, y).
Axes of the slice: x: 2, y: 2, z: 4, core: 2. Of those that a mesh axis runs over, the one named last changes fastest.
Arguments:
- fields: float32 [24, 64, 128, 128], P(None, ('grp', 'dev')), may hold values from -6 to 6
- mix_matrix: float32 [24, 24], replicated, may hold values from -1.25 to 1.25
- laplace_matrix: float32 [24, 24], replicated, may hold values from -0.21875 to 0.21875
Outputs:
- rhs: float32 [24, 64, 128, 128], P(None, ('grp', 'dev'))
- weyl: float32 [2, 64, 128, 128], P(None, 'grp', 'dev')
All inputs are finite; a program needn't handle non-finite values.
Results may differ from a plain program's by a relative error of at most 0.0003.
Values sent between devices are 32-bit elements; how exact they have to be, the bound alone decides.
A program may use at most 192 MiB of HBM per device.

v0:
```python
import jax
import jax.numpy as jnp
from jax import lax
from jax.sharding import PartitionSpec as P


def with_halo(block, sides, width):
    for axis, dim in sides:
        count = lax.axis_size(axis)
        forward = [(i, i + 1) for i in range(count - 1)]
        forward.append((count - 1, 0))
        backward = [(target, source) for source, target in forward]
        low = lax.ppermute(
            lax.slice_in_dim(block, block.shape[dim] - width, None, axis=dim), axis, forward
        )
        high = lax.ppermute(lax.slice_in_dim(block, 0, width, axis=dim), axis, backward)
        block = jnp.concatenate([low, block, high], axis=dim)
    return block


def pad_periodic(field, dimension):
    length = field.shape[dimension]
    before = lax.slice_in_dim(field, length - 2, length, axis=dimension)
    after = lax.slice_in_dim(field, 0, 2, axis=dimension)
    return jnp.concatenate([before, field, after], axis=dimension)


def interior(padded, keep):
    result = padded
    for dimension in (1, 2, 3):
        if dimension != keep:
            result = lax.slice_in_dim(result, 2, result.shape[dimension] - 2, axis=dimension)
    return result


def stencil_values(padded, dimension):
    centre = interior(padded, dimension)
    length = centre.shape[dimension] - 4
    return [
        lax.slice_in_dim(centre, offset, offset + length, axis=dimension) for offset in range(5)
    ]


def first_diff(padded, dimension):
    values = stencil_values(padded, dimension)
    return (values[0] - 8.0 * values[1] + 8.0 * values[3] - values[4]) / 12.0


def second_diff(padded, dimension):
    values = stencil_values(padded, dimension)
    return (-values[0] + 16.0 * values[1] - 30.0 * values[2] + 16.0 * values[3] - values[4]) / 12.0


def laplacian(padded):
    return second_diff(padded, 1) + second_diff(padded, 2) + second_diff(padded, 3)


def evolution(padded, mix_matrix, laplace_matrix):
    centre = interior(padded, 0)
    laplace = laplacian(padded)
    result = jnp.einsum("fg,gzyx->fzyx", mix_matrix, centre, precision=lax.Precision.HIGHEST)
    result = result + jnp.einsum(
        "fg,gzyx->fzyx", laplace_matrix, laplace, precision=lax.Precision.HIGHEST
    )
    for dimension in (1, 2, 3):
        result = result + centre[11 + dimension][None] * first_diff(padded, dimension)
    return result


def contract(tensor, left, right):
    total = 0.0
    for first in range(3):
        for second in range(3):
            total = total + tensor[first][second] * left[first] * right[second]
    return total


def weyl_scalar(padded, zpos, ypos, xpos):
    table = ((0, 1, 2), (1, 3, 4), (2, 4, 5))
    metric = padded[0:6]
    curv_padded = padded[6:12]
    lap_metric = laplacian(metric)
    curvature = interior(curv_padded, 0)
    gradient = [first_diff(curv_padded, 3 - index) for index in range(3)]
    trace = curvature[0] + curvature[3] + curvature[5]
    electric = []
    curl = []
    for first in range(3):
        erow = []
        crow = []
        for second in range(3):
            value = (
                -0.5 * lap_metric[table[first][second]] - trace * curvature[table[first][second]]
            )
            for middle in range(3):
                value = value + curvature[table[first][middle]] * curvature[table[middle][second]]
            erow.append(value)
            next_one = (first + 1) % 3
            next_two = (first + 2) % 3
            crow.append(
                gradient[next_one][table[next_two][second]]
                - gradient[next_two][table[next_one][second]]
            )
        electric.append(erow)
        curl.append(crow)
    magnetic = [
        [0.5 * (curl[first][second] + curl[second][first]) for second in range(3)]
        for first in range(3)
    ]
    along_x = xpos[None, None, :]
    along_y = ypos[None, :, None]
    along_z = zpos[:, None, None]
    cylinder = jnp.sqrt(along_x * along_x + along_y * along_y)
    radius = jnp.sqrt(cylinder * cylinder + along_z * along_z)
    theta_vec = (
        along_z * along_x / (radius * cylinder),
        along_z * along_y / (radius * cylinder),
        -cylinder / radius,
    )
    phi_vec = (-along_y / cylinder, along_x / cylinder, 0.0)
    real_part = 0.5 * (
        contract(electric, theta_vec, theta_vec) - contract(electric, phi_vec, phi_vec)
    ) - contract(magnetic, theta_vec, phi_vec)
    imag_part = -contract(electric, theta_vec, phi_vec) - 0.5 * (
        contract(magnetic, theta_vec, theta_vec) - contract(magnetic, phi_vec, phi_vec)
    )
    return jnp.stack([real_part, imag_part])


def centred(index, count):
    return index.astype(jnp.float32) + 0.5 - 0.5 * count


def per_device(fields, mix_matrix, laplace_matrix):
    depth = fields.shape[1]
    rows = fields.shape[2]
    width = fields.shape[3]
    groups = lax.axis_size("grp")
    members = lax.axis_size("dev")
    total_depth = depth * groups * members
    slab = lax.axis_index("grp") * members + lax.axis_index("dev")
    zpadded = with_halo(fields, ((("grp", "dev"), 1),), 2)
    padded = pad_periodic(pad_periodic(zpadded, 2), 3)
    rhs = evolution(padded, mix_matrix, laplace_matrix)
    xpos = centred(jnp.arange(width, dtype=jnp.int32), width)
    zpos = centred(slab * depth + jnp.arange(depth, dtype=jnp.int32), total_depth)
    ypos = centred(jnp.arange(rows, dtype=jnp.int32), rows)
    local = weyl_scalar(padded[0:12], zpos, ypos, xpos)
    weyl = lax.all_to_all(local, "dev", split_axis=2, concat_axis=1, tiled=True)
    return (rhs, weyl)


def solution(mesh):
    return jax.shard_map(
        per_device,
        mesh=mesh,
        in_specs=(P(None, ("grp", "dev"), None, None), P(), P()),
        out_specs=(P(None, ("grp", "dev"), None, None), P(None, "grp", "dev", None)),
        check_vma=False,
    )
```

profile of v0, /device:TPU:0, one launch (start us, length us, event | category | flops | bytes accessed | tf_op | source)
XLA Modules:
  0.0 235.9 jit_solution(244997973038235878)
XLA Ops:
  0.6 3.1 %collective-permute-start = (f32[24,2,128,128]{3,2,1,0:T(8,128)}, f32[24,2,128,128]{3,2,1,0:T(8,128)S(1)}, u32[]{:S(2)}, u32[]{:S(2)}) collective-permute-start(f32[24,2,128,128]{3,2,1,0:T(8,128)} %param.3), channel_id=1, source_target_pairs={{0,1},{1,2},{2,3},{3,4},{4,5},{5,6},{6,7},{7,8},{8,9},{9,10},{10,1... | collective-permute-start | bytes 9437192 | tf_op jit(solution)/shard_map/ppermute | solution.py:13
  3.7 3.5 %collective-permute-start.1 = (f32[24,2,128,128]{3,2,1,0:T(8,128)}, f32[24,2,128,128]{3,2,1,0:T(8,128)}, u32[]{:S(2)}, u32[]{:S(2)}) collective-permute-start(f32[24,2,128,128]{3,2,1,0:T(8,128)} %param.3), channel_id=1, source_target_pairs={{1,0},{2,1},{3,2},{4,3},{5,4},{6,5},{7,6},{8,7},{9,8},{10,9},{11,1... | collective-permute-start | bytes 9437192 | tf_op jit(solution)/shard_map/ppermute | solution.py:16
  7.2 0.1 broadcast_multiply_fusion
  7.3 2.0 add_add_fusion
  9.3 0.9 fusion.118
  10.1 7.7 %fusion.9 = f32[24,2,128,128]{3,0,2,1:T(8,128)} fusion(f32[24,2,128,128]{3,2,1,0:T(8,128)} %param.3, f32[24,24]{1,0:T(8,128)S(1)} %copy-done), kind=kOutput, calls=%fused_computation.35 | convolution fusion | flops 226492416 | bytes 6293760 | tf_op jit(solution)/shard_map/fg,gzyx->fzyx/dot_general | solution.py:61
  17.9 120.9 %collective-permute-done = f32[24,2,128,128]{3,2,1,0:T(8,128)S(1)} collective-permute-done((f32[24,2,128,128]{3,2,1,0:T(8,128)}, f32[24,2,128,128]{3,2,1,0:T(8,128)S(1)}, u32[]{:S(2)}, u32[]{:S(2)}) %collective-permute-start) | collective-permute-done | bytes 3145760 | tf_op jit(solution)/shard_map/ppermute | solution.py:13
  138.8 0.6 constant_dynamic-update-slice_fusion.6
  139.4 0.9 constant_dynamic-update-slice_fusion.5
  140.3 0.7 collective-permute-done.1
  141.0 4.1 %constant_dynamic-update-slice_fusion.4 = (f32[24,6,128,128]{3,2,1,0:T(8,128)S(1)}, f32[24,4,128,128]{3,2,1,0:T(8,128)S(1)}) fusion(f32[24,6,128,128]{3,2,1,0:T(8,128)S(1)} %get-tuple-element.31, f32[24,2,128,128]{3,2,1,0:T(8,128)} %collective-permute-done.1, f32[24,4,128,128]{3,2,1,0:T(8,128)S(1)} %get-tuple-element.32), kind=kLoop, calls=%fused_computation.203 | loop fusion | bytes 9437184 | tf_op jit(solution)/shard_map/concatenate | solution.py:17
  145.1 2.6 %copy-done.7 = f32[24,4,128,128]{3,2,1,0:T(8,128)} copy-done((f32[24,4,128,128]{3,2,1,0:T(8,128)}, f32[24,4,128,128]{3,2,1,0:T(8,128)S(1)}, u32[]{:S(2)}) %copy-start.7) | copy-done | bytes 6291480
  147.7 0.1 fusion.137
  147.8 5.7 %pad_maximum_fusion = f32[24,6,132,128]{3,2,1,0:T(8,128)} fusion(f32[24,6,2,128]{3,2,1,0:T(2,128)S(1)} %get-tuple-element.23, f32[24,6,128,128]{3,2,1,0:T(8,128)S(1)} %get-tuple-element.29, f32[24,6,2,128]{3,2,1,0:T(2,128)S(1)} %get-tuple-element.24), kind=kLoop, calls=%fused_computation.10 | loop fusion | flops 4866048 | bytes 19464192 | tf_op jit(solution)/shard_map/concatenate | solution.py:25
  153.5 14.3 %fusion.136 = (f32[24,6,132,2]{3,2,1,0:T(8,128)S(1)}, f32[24,6,132,2]{3,2,1,0:T(8,128)}) fusion(f32[24,6,132,128]{3,2,1,0:T(8,128)} %pad_maximum_fusion), kind=kLoop, calls=%fused_computation.214 | loop fusion | bytes 608256 | tf_op jit(solution)/shard_map/slice | solution.py:24
  167.8 4.4 %fusion.31 = f32[6,2,128,128]{3,2,1,0:T(8,128)S(1)} fusion(f32[24,6,132,2]{3,2,1,0:T(8,128)S(1)} %get-tuple-element.21, f32[24,6,2,128]{3,2,1,0:T(2,128)S(1)} %get-tuple-element.23, f32[24,6,128,128]{3,2,1,0:T(8,128)S(1)} %get-tuple-element.29, f32[24,6,2,128]{3,2,1,0:T(2,128)S(1)} %get-tuple-element.24, f32[24,6,132,2]{3,2,1,0:T(8,128)} %get-tuple-element.22), kind=kLoop, calls=%fused_computation.59 | loop fusion | flops 3538944 | bytes 10822656 | tf_op jit(solution)/shard_map/div | solution.py:46
  172.1 0.7 copy-done.3
  172.8 1.2 slice-done.3
  174.1 1.3 slice-done.4
  175.3 0.4 slice-done.5
  175.8 3.7 %fusion.46 = f32[6,2,128,128]{3,2,1,0:T(8,128)S(1)} fusion(f32[24,6,132,2]{3,2,1,0:T(8,128)S(1)} %get-tuple-element.21, f32[24,6,2,128]{3,2,1,0:T(2,128)S(1)} %get-tuple-element.23, f32[24,6,128,128]{3,2,1,0:T(8,128)S(1)} %get-tuple-element.29, f32[24,6,2,128]{3,2,1,0:T(2,128)S(1)} %get-tuple-element.24, f32[24,6,132,2]{3,2,1,0:T(8,128)S(1)} %bitcast.31, ...), kind=kLoop, calls=%fused_computation.93 | loop fusion | flops 8060928 | bytes 14754816 | tf_op jit(solution)/shard_map/add | solution.py:55
  179.6 2.3 fusion.35
  182.0 0.7 fusion.72
  182.7 0.0 copy-done.17
  182.8 0.0 copy-done.18
  182.8 0.5 fusion.82
  183.3 0.9 copy.42
  184.2 6.9 %all-to-all-start = ((f32[2,2,128,128]{3,0,1,2:T(2,128)}), f32[2,2,128,128]{3,0,1,2:T(2,128)}, u32[]{:S(2)}, u32[]{:S(2)}) async-start(f32[2,2,128,128]{3,0,1,2:T(2,128)} %copy.42), calls=%async_computation | async-start | bytes 524288 | tf_op jit(solution)/shard_map/all_to_all | solution.py:149
  191.1 25.8 %add_multiply_fusion = (f32[24,2,128,128]{3,2,1,0:T(8,128)}, f32[24,2,128,128]{3,2,1,0:T(8,128)}, f32[24,2,128,128]{3,2,1,0:T(8,128)}, f32[24,2,128,128]{3,2,1,0:T(8,128)}, f32[24,2,128,128]{3,2,1,0:T(8,128)}) fusion(f32[24,2,128,128]{3,2,1,0:T(8,128)} %collective-permute-done.1, f32[24,2,128,128]{3,2,1,0:T(8,128)} %param.3, ...), kind=kLoop, calls=%fused_computation.37 | loop fusion | flops 32243712 | bytes 41493504 | tf_op jit(solution)/shard_map/add | solution.py:55
  216.9 6.6 %fusion.7 = f32[2,128,128,24]{2,3,1,0:T(8,128)S(1)} fusion(f32[24,2,128,128]{3,2,1,0:T(8,128)} %get-tuple-element.16, f32[24,24]{1,0:T(8,128)S(1)} %copy-done.19), kind=kOutput, calls=%fused_computation.33 | convolution fusion | flops 226492416 | bytes 6293760 | tf_op jit(solution)/shard_map/fg,gzyx->fzyx/dot_general | solution.py:62
  223.6 10.6 %fusion.6 = f32[24,2,128,128]{3,2,1,0:T(8,128)} fusion(f32[24,2,128,128]{3,0,2,1:T(8,128)} %fusion.9, f32[2,128,128,24]{2,3,1,0:T(8,128)S(1)} %fusion.7, f32[24,2,128,128]{3,2,1,0:T(8,128)} %get-tuple-element.20, f32[24,2,128,128]{3,2,1,0:T(8,128)} %get-tuple-element.19, f32[24,2,128,128]{3,2,1,0:T(8,128)S(1)} %copy-done.9, ...), kind=kLoop, calls=%fused_computation.32 | loop fusion | flops 20447232 | bytes 44728320 | tf_op jit(solution)/shard_map/add | solution.py:66
  234.2 1.7 copy.43
  (52 shorter events, 0.1 us)
Async XLA Ops:
  0.6 9.5 %copy-start = (f32[24,24]{1,0:T(8,128)S(1)}, f32[24,24]{1,0:T(8,128)}, u32[]{:S(2)}) copy-start(f32[24,24]{1,0:T(8,128)} %param.4) | copy-start | bytes 6916
  0.6 138.1 %collective-permute-start = (f32[24,2,128,128]{3,2,1,0:T(8,128)}, f32[24,2,128,128]{3,2,1,0:T(8,128)S(1)}, u32[]{:S(2)}, u32[]{:S(2)}) collective-permute-start(f32[24,2,128,128]{3,2,1,0:T(8,128)} %param.3), channel_id=1, source_target_pairs={{0,1},{1,2},{2,3},{3,4},{4,5},{5,6},{6,7},{7,8},{8,9},{9,10},{10,1... | collective-permute-start | bytes 9437192 | tf_op jit(solution)/shard_map/ppermute | solution.py:13
  3.7 137.3 %collective-permute-start.1 = (f32[24,2,128,128]{3,2,1,0:T(8,128)}, f32[24,2,128,128]{3,2,1,0:T(8,128)}, u32[]{:S(2)}, u32[]{:S(2)}) collective-permute-start(f32[24,2,128,128]{3,2,1,0:T(8,128)} %param.3), channel_id=1, source_target_pairs={{1,0},{2,1},{3,2},{4,3},{5,4},{6,5},{7,6},{8,7},{9,8},{10,9},{11,1... | collective-permute-start | bytes 9437192 | tf_op jit(solution)/shard_map/ppermute | solution.py:16
  17.9 121.5 %copy-start.4 = (f32[24,2,128,128]{3,2,1,0:T(8,128)S(1)}, f32[24,2,128,128]{3,2,1,0:T(8,128)}, u32[]{:S(2)}) copy-start(f32[24,2,128,128]{3,2,1,0:T(8,128)} %param.3) | copy-start | bytes 9437188
  138.8 40.7 %copy-start.5 = (f32[24,2,128,128]{3,2,1,0:T(8,128)}, f32[24,2,128,128]{3,2,1,0:T(8,128)S(1)}, u32[]{:S(2)}) copy-start(f32[24,2,128,128]{3,2,1,0:T(8,128)S(1)} %collective-permute-done) | copy-start | bytes 9437188
  140.3 4.8 %copy-start.8 = (f32[24,4,128,128]{3,2,1,0:T(8,128)}, f32[24,4,128,128]{3,2,1,0:T(8,128)S(1)}, u32[]{:S(2)}) copy-start(f32[24,4,128,128]{3,2,1,0:T(8,128)S(1)} %get-tuple-element.33) | copy-start | bytes 18874372
  145.1 2.6 %copy-start.7 = (f32[24,4,128,128]{3,2,1,0:T(8,128)}, f32[24,4,128,128]{3,2,1,0:T(8,128)S(1)}, u32[]{:S(2)}) copy-start(f32[24,4,128,128]{3,2,1,0:T(8,128)S(1)} %get-tuple-element.30) | copy-start | bytes 18874372
  147.7 31.8 %copy-start.2 = (f32[24,6,128,128]{3,2,1,0:T(8,128)}, f32[24,6,128,128]{3,2,1,0:T(8,128)S(1)}, u32[]{:S(2)}) copy-start(f32[24,6,128,128]{3,2,1,0:T(8,128)S(1)} %get-tuple-element.29) | copy-start | bytes 28311556
  167.8 5.1 %copy-start.3 = (f32[24,6,132,2]{3,2,1,0:T(8,128)}, f32[24,6,132,2]{3,2,1,0:T(8,128)S(1)}, u32[]{:S(2)}) copy-start(f32[24,6,132,2]{3,2,1,0:T(8,128)S(1)} %get-tuple-element.21) | copy-start | bytes 456196
  167.8 6.3 %slice-start.3 = ((s8[10027008]{0:T(1024)(128)(4,1)}), s8[4194304]{0:T(1024)(128)(4,1)S(1)}, s32[]{:S(2)}) async-start(s8[10027008]{0:T(1024)(128)(4,1)} %bitcast.30), calls=%async_computation.4 | async-start | bytes 8388608
  167.8 7.6 %slice-start.4 = ((s8[10027008]{0:T(1024)(128)(4,1)}), s8[4194304]{0:T(1024)(128)(4,1)S(1)}, s32[]{:S(2)}) async-start(s8[10027008]{0:T(1024)(128)(4,1)} %bitcast.30), calls=%async_computation.5 | async-start | bytes 8388608
  167.8 8.0 %slice-start.5 = ((s8[10027008]{0:T(1024)(128)(4,1)}), s8[1638400]{0:T(1024)(128)(4,1)S(1)}, s32[]{:S(2)}) async-start(s8[10027008]{0:T(1024)(128)(4,1)} %bitcast.30), calls=%async_computation.6 | async-start | bytes 3276800
  179.5 2.4 %copy-start.11 = (f32[128,128]{1,0:T(8,128)S(1)}, f32[128,128]{1,0:T(8,128)}, u32[]{:S(2)}) copy-start(f32[128,128]{1,0:T(8,128)} %get-tuple-element.42) | copy-start | bytes 196612
  179.5 2.4 %copy-start.12 = (f32[128,128]{1,0:T(8,128)S(1)}, f32[128,128]{1,0:T(8,128)}, u32[]{:S(2)}) copy-start(f32[128,128]{1,0:T(8,128)} %get-tuple-element.43) | copy-start | bytes 196612
  179.6 2.4 %copy-start.13 = (f32[128,128]{1,0:T(8,128)S(1)}, f32[128,128]{1,0:T(8,128)}, u32[]{:S(2)}) copy-start(f32[128,128]{1,0:T(8,128)} %get-tuple-element.44) | copy-start | bytes 196612
  179.6 2.4 %copy-start.14 = (f32[128,128]{1,0:T(8,128)S(1)}, f32[128,128]{1,0:T(8,128)}, u32[]{:S(2)}) copy-start(f32[128,128]{1,0:T(8,128)} %get-tuple-element.45) | copy-start | bytes 196612
  179.6 2.4 %copy-start.15 = (f32[128,128]{1,0:T(8,128)S(1)}, f32[128,128]{1,0:T(8,128)}, u32[]{:S(2)}) copy-start(f32[128,128]{1,0:T(8,128)} %get-tuple-element.47) | copy-start | bytes 196612
  179.6 2.4 %copy-start.16 = (f32[1,2,128,128]{3,2,1,0:T(8,128)S(1)}, f32[1,2,128,128]{3,2,1,0:T(8,128)}, u32[]{:S(2)}) copy-start(f32[1,2,128,128]{3,2,1,0:T(8,128)} %get-tuple-element.25) | copy-start | bytes 393220
  181.9 0.8 copy-start.17
  181.9 0.9 copy-start.18
  184.2 39.3 %slice-start = ((s8[9437184]{0:T(1024)(128)(4,1)}), s8[1048576]{0:T(1024)(128)(4,1)S(1)}, s32[]{:S(2)}) async-start(s8[9437184]{0:T(1024)(128)(4,1)} %bitcast.28), calls=%async_computation.1 | async-start | bytes 2097152
  184.2 49.9 %all-to-all-start = ((f32[2,2,128,128]{3,0,1,2:T(2,128)}), f32[2,2,128,128]{3,0,1,2:T(2,128)}, u32[]{:S(2)}, u32[]{:S(2)}) async-start(f32[2,2,128,128]{3,0,1,2:T(2,128)} %copy.42), calls=%async_computation | async-start | bytes 524288 | tf_op jit(solution)/shard_map/all_to_all | solution.py:149
  191.1 25.8 %copy-start.19 = (f32[24,24]{1,0:T(8,128)S(1)}, f32[24,24]{1,0:T(8,128)}, u32[]{:S(2)}) copy-start(f32[24,24]{1,0:T(8,128)} %param.5) | copy-start | bytes 6916
  191.1 32.4 %slice-start.1 = ((s8[9437184]{0:T(1024)(128)(4,1)}), s8[4194304]{0:T(1024)(128)(4,1)S(1)}, s32[]{:S(2)}) async-start(s8[9437184]{0:T(1024)(128)(4,1)} %bitcast.28), calls=%async_computation.2 | async-start | bytes 8388608
  191.1 32.4 %slice-start.2 = ((s8[9437184]{0:T(1024)(128)(4,1)}), s8[4194304]{0:T(1024)(128)(4,1)S(1)}, s32[]{:S(2)}) async-start(s8[9437184]{0:T(1024)(128)(4,1)} %bitcast.28), calls=%async_computation.3 | async-start | bytes 8388608
  216.9 6.6 %copy-start.6 = (f32[24,2,128,128]{3,2,1,0:T(8,128)S(1)}, f32[24,2,128,128]{3,2,1,0:T(8,128)}, u32[]{:S(2)}) copy-start(f32[24,2,128,128]{3,2,1,0:T(8,128)} %copy-done.5) | copy-start | bytes 9437188
  216.9 6.6 %copy-start.9 = (f32[24,2,128,128]{3,2,1,0:T(8,128)S(1)}, f32[24,2,128,128]{3,2,1,0:T(8,128)}, u32[]{:S(2)}) copy-start(f32[24,2,128,128]{3,2,1,0:T(8,128)} %get-tuple-element.17) | copy-start | bytes 9437188
  216.9 6.6 %copy-start.10 = (f32[24,2,128,128]{3,2,1,0:T(8,128)S(1)}, f32[24,2,128,128]{3,2,1,0:T(8,128)}, u32[]{:S(2)}) copy-start(f32[24,2,128,128]{3,2,1,0:T(8,128)} %get-tuple-element.18) | copy-start | bytes 9437188
  223.6 12.3 %copy-start.1 = (f32[24,24]{1,0:T(8,128)S(1)}, f32[24,24]{1,0:T(8,128)}, u32[]{:S(2)}) copy-start(f32[24,24]{1,0:T(8,128)} %param.4) | copy-start | bytes 6916
where the time goes:
time: 236 us
  waiting for transfers between devices  122 us (52%)
  other arithmetic  56.6 us (24%)
  local copies, waits for them, and re-layouts  28.9 us (12%)
  matrix products  14.3 us (6%)
  starting transfers between devices  13.4 us (6%)
    ppermute x1, waiting for transfers between devices, with_halo(): lax.ppermute(lax.slice_in_dim(block, block.shape[dim] - width, None, axis...  121 us
    add x2, other arithmetic, laplacian(): second_diff(padded, 1) + second_diff(padded, 2) + second_diff(padded, 3)  29.5 us
    slice x2, local copies, waits for them, and re-layouts, pad_periodic(): after = lax.slice_in_dim(field, 0, 2, axis=dimension)  14.4 us
    add x1, other arithmetic, evolution(): result + centre[11 + dimension][None] * first_diff(padded, dimension)  10.6 us
    unnamed x54, local copies, waits for them, and re-layouts  7.89 us
    dot_general x1, matrix products, evolution(): jnp.einsum('fg,gzyx->fzyx', mix_matrix, centre, precision=lax.Precision.H...  7.73 us
    all_to_all x1, starting transfers between devices, per_device(): weyl = lax.all_to_all(local, 'dev', split_axis=2, concat_axis=1, tiled=True)  6.88 us
    div x2, other arithmetic, first_diff(): return (values[0] - 8.0 * values[1] + 8.0 * values[3] - values[4]) / 12.0  6.67 us
  transfers between devices with their start and end apart: 3, of which 2 were waited for; matrix products, arithmetic and copies ran while one was open for 23% of the time, Pallas kernels for 0%

commit v1 on v0

v1 whole, which is shorter than its diff:
```python
import functools

import jax
import jax.numpy as jnp
from jax import lax
from jax.experimental import pallas as pl
from jax.experimental.pallas import tpu as pltpu
from jax.sharding import PartitionSpec as P

AHEAD = 12
LAG = 3
TABLE = ((0, 1, 2), (1, 3, 4), (2, 4, 5))
PAIRS = ((0, 0), (0, 1), (0, 2), (1, 1), (1, 2), (2, 2))


def contract(tensor, left, right):
    total = None
    for first in range(3):
        for second in range(3):
            if left[first] is None or right[second] is None:
                continue
            term = tensor[TABLE[first][second]] * (left[first] * right[second])
            total = term if total is None else total + term
    return total


def weyl_pair(curv, lap, grad, along_x, along_y, along_z):
    trace = curv[0] + curv[3] + curv[5]
    electric = []
    for first, second in PAIRS:
        spot = TABLE[first][second]
        value = -0.5 * lap[spot] - trace * curv[spot]
        for middle in range(3):
            value = value + curv[TABLE[first][middle]] * curv[TABLE[middle][second]]
        electric.append(value)

    def curl(first, second):
        one = (first + 1) % 3
        two = (first + 2) % 3
        return grad[one][TABLE[two][second]] - grad[two][TABLE[one][second]]

    magnetic = [0.5 * (curl(first, second) + curl(second, first)) for first, second in PAIRS]
    square = along_x * along_x + along_y * along_y
    cylinder = jnp.sqrt(square)
    radius = jnp.sqrt(square + along_z * along_z)
    over_cyl = 1.0 / cylinder
    over_rad = 1.0 / radius
    slope = along_z * over_rad * over_cyl
    theta = (slope * along_x, slope * along_y, -cylinder * over_rad)
    phi = (-along_y * over_cyl, along_x * over_cyl, None)
    real = 0.5 * (contract(electric, theta, theta) - contract(electric, phi, phi)) - contract(
        magnetic, theta, phi
    )
    imag = -contract(electric, theta, phi) - 0.5 * (
        contract(magnetic, theta, theta) - contract(magnetic, phi, phi)
    )
    return real, imag


def kernel(
    groups,
    members,
    fields_ref,
    mix_ref,
    lap_ref,
    rhs_ref,
    weyl_ref,
    own,
    halo,
    lapbuf,
    laph,
    gradk,
    wtmp,
    wloc,
    wrecv,
    own_sem,
    send_p,
    recv_p,
    send_r,
    recv_r,
    send_w,
    recv_w,
):
    count, depth, rows, width = own.shape
    slabs = groups * members
    grp = lax.axis_index("grp")
    dev = lax.axis_index("dev")
    slab = grp * members + dev
    side = lax.rem(slab, 2)
    partner = slab + 1 - 2 * side
    follow = lax.rem(slab + slabs + 2 - 4 * side, slabs)
    other = lax.rem(slab + slabs - 2 + 4 * side, slabs)
    per = rows // members

    def place(index):
        return (index // members, lax.rem(index, members))

    load = pltpu.make_async_copy(fields_ref, own, own_sem)
    load.start()

    def peer(offset):
        return lax.rem(dev + offset, members)

    barrier = pltpu.get_barrier_semaphore()
    for target in (follow, other):
        pl.semaphore_signal(
            barrier, inc=1, device_id=place(target), device_id_type=pl.DeviceIdType.MESH
        )
    for offset in range(1, members):
        pl.semaphore_signal(
            barrier, inc=1, device_id=(grp, peer(offset)), device_id_type=pl.DeviceIdType.MESH
        )
    pl.semaphore_wait(barrier, members + 1)

    def exchange(i, slot):
        return pltpu.make_async_remote_copy(
            src_ref=fields_ref.at[i],
            dst_ref=halo.at[slot, i],
            send_sem=send_p.at[i],
            recv_sem=recv_p.at[i],
            device_id=place(partner),
            device_id_type=pl.DeviceIdType.MESH,
        )

    def relay(i, slot):
        return pltpu.make_async_remote_copy(
            src_ref=halo.at[1 - side, i],
            dst_ref=halo.at[slot, i],
            send_sem=send_r.at[i],
            recv_sem=recv_r.at[i],
            device_id=place(follow),
            device_id_type=pl.DeviceIdType.MESH,
        )

    def spread(target, source):
        return pltpu.make_async_remote_copy(
            src_ref=wloc.at[target],
            dst_ref=wrecv.at[source],
            send_sem=send_w.at[target],
            recv_sem=recv_w.at[source],
            device_id=(grp, target),
            device_id_type=pl.DeviceIdType.MESH,
        )

    ahead = min(AHEAD, count)

    @pl.loop(0, ahead)
    def _(i):
        exchange(i, side).start()

    rhs_ref[...] = jnp.zeros_like(rhs_ref)
    load.wait()

    def advance(i):
        exchange(i, 1 - side).wait_recv()
        relay(i, side).start()

        @pl.when(i + ahead < count)
        def _():
            exchange(i + ahead, side).start()

    @pl.loop(0, LAG)
    def _(i):
        advance(i)

    def weyl_local():
        tiles = rows // 8

        @pl.loop(0, depth * tiles)
        def _(t):
            p = t // tiles
            start = pl.multiple_of(lax.rem(t, tiles) * 8, 8)
            strip = pl.ds(start, 8)
            curv = [own[6 + n, p, strip, :] for n in range(6)]
            lap = [laph[n, p, strip, :] for n in range(6)]
            grad = [[gradk[n, a, p, strip, :] for n in range(6)] for a in range(3)]
            lane = lax.broadcasted_iota(jnp.int32, (8, width), 1)
            row = lax.broadcasted_iota(jnp.int32, (8, width), 0) + start
            layer = jnp.full((8, width), slab * depth + p, jnp.int32)
            along_x = lane.astype(jnp.float32) + (0.5 - 0.5 * width)
            along_y = row.astype(jnp.float32) + (0.5 - 0.5 * rows)
            along_z = layer.astype(jnp.float32) + (0.5 - 0.5 * depth * slabs)
            real, imag = weyl_pair(curv, lap, grad, along_x, along_y, along_z)
            wtmp[0, p, strip, :] = real
            wtmp[1, p, strip, :] = imag

        for m in range(members):
            wloc[m] = wtmp[:, :, m * per : (m + 1) * per, :]

    def process(g):
        for p in range(depth):
            f = own[g, p]
            planes = [halo[0, g, 0], halo[0, g, 1], own[g, 0], own[g, 1], halo[1, g, 0], halo[1, g, 1]]
            zm2, zm1, _, zp1, zp2 = planes[p : p + 5]
            ym1, ym2 = pltpu.roll(f, 1, 0), pltpu.roll(f, 2, 0)
            yp1, yp2 = pltpu.roll(f, rows - 1, 0), pltpu.roll(f, rows - 2, 0)
            xm1, xm2 = pltpu.roll(f, 1, 1), pltpu.roll(f, 2, 1)
            xp1, xp2 = pltpu.roll(f, width - 1, 1), pltpu.roll(f, width - 2, 1)
            near = ((zm1 + zp1) + (ym1 + yp1)) + (xm1 + xp1)
            far = ((zm2 + zp2) + (ym2 + yp2)) + (xm2 + xp2)
            lap = (16.0 * near - far - 90.0 * f) * (1.0 / 12.0)
            lapbuf[p] = lap
            gz = (8.0 * (zp1 - zm1) - (zp2 - zm2)) * (1.0 / 12.0)
            gy = (8.0 * (yp1 - ym1) - (yp2 - ym2)) * (1.0 / 12.0)
            gx = (8.0 * (xp1 - xm1) - (xp2 - xm2)) * (1.0 / 12.0)
            rhs_ref[g, p] += own[12, p] * gz + own[13, p] * gy + own[14, p] * gx

            @pl.when(g < 6)
            def _():
                laph[g, p] = lap

            @pl.when(jnp.logical_and(g >= 6, g < 12))
            def _():
                gradk[g - 6, 0, p] = gx
                gradk[g - 6, 1, p] = gy
                gradk[g - 6, 2, p] = gz

        step = 32

        @pl.loop(0, depth * (rows // step))
        def _(t):
            p = t // (rows // step)
            strip = pl.ds(pl.multiple_of(lax.rem(t, rows // step) * step, step), step)
            f = own[g, p, strip, :]
            lap = lapbuf[p, strip, :]
            for c in range(count):
                rhs_ref[c, p, strip, :] += mix_ref[c, g] * f + lap_ref[c, g] * lap

    @pl.loop(0, count)
    def _(g):
        @pl.when(g + LAG < count)
        def _():
            advance(g + LAG)

        relay(g, side).wait_recv()
        process(g)

        @pl.when(g == 11)
        def _():
            weyl_local()

        @pl.when(g == 13)
        def _():
            for offset in range(1, members):
                spread(peer(offset), dev).start()

    def put(source, block):
        for comp in range(2):
            for p in range(depth):
                weyl_ref[comp, source * depth + p] = block[comp, p]

    put(dev, wloc.at[dev])
    for offset in range(1, members):
        source = peer(offset)
        spread(source, source).wait_recv()
        put(source, wrecv.at[source])
    for offset in range(1, members):
        spread(peer(offset), dev).wait_send()

    @pl.loop(0, count)
    def _(i):
        exchange(i, side).wait_send()
        relay(i, side).wait_send()


def per_device(groups, members, fields, mix_matrix, laplace_matrix):
    count, depth, rows, width = fields.shape
    assert depth == 2 and (groups * members) % 2 == 0 and members % 2 == 0
    plane = (rows, width)
    per = rows // members
    vmem = functools.partial(pltpu.VMEM, dtype=jnp.float32)
    dma = pltpu.SemaphoreType.DMA
    return pl.pallas_call(
        functools.partial(kernel, groups, members),
        out_shape=(
            jax.ShapeDtypeStruct(fields.shape, jnp.float32),
            jax.ShapeDtypeStruct((2, depth * members, per, width), jnp.float32),
        ),
        in_specs=[
            pl.BlockSpec(memory_space=pl.ANY),
            pl.BlockSpec(memory_space=pltpu.SMEM),
            pl.BlockSpec(memory_space=pltpu.SMEM),
        ],
        out_specs=(
            pl.BlockSpec(memory_space=pltpu.VMEM),
            pl.BlockSpec(memory_space=pltpu.VMEM),
        ),
        scratch_shapes=[
            vmem((count, depth) + plane),
            vmem((2, count, depth) + plane),
            vmem((depth,) + plane),
            vmem((6, depth) + plane),
            vmem((6, 3, depth) + plane),
            vmem((2, depth) + plane),
            vmem((members, 2, depth, per, width)),
            vmem((members, 2, depth, per, width)),
            dma,
            dma((count,)),
            dma((count,)),
            dma((count,)),
            dma((count,)),
            dma((members,)),
            dma((members,)),
        ],
        compiler_params=pltpu.CompilerParams(
            collective_id=0, has_side_effects=True, vmem_limit_bytes=48 * 1024 * 1024
        ),
        name="evolve",
    )(fields, mix_matrix, laplace_matrix)


def solution(mesh):
    groups, members = mesh.shape["grp"], mesh.shape["dev"]
    return jax.shard_map(
        functools.partial(per_device, groups, members),
        mesh=mesh,
        in_specs=(P(None, ("grp", "dev"), None, None), P(), P()),
        out_specs=(P(None, ("grp", "dev"), None, None), P(None, "grp", "dev", None)),
        check_vma=False,
    )
```

time: 236 us -> 91.7 us (0.39)
  waiting for transfers between devices: 122 us -> 0 us
  Pallas kernels: 0 us -> 86.2 us
  other arithmetic: 56.6 us -> 0 us
  local copies, waits for them, and re-layouts: 28.9 us -> 3.78 us
  matrix products: 14.3 us -> 0 us
  starting transfers between devices: 13.4 us -> 0 us
    ppermute x2 -> x0, waiting for transfers between devices: 122 us -> none  [the longest x1 121 us: with_halo(): lax.ppermute(lax.slice_in_dim(block, block.shape[dim] - width, None, axis...]
    pallas_call x0 -> x1, Pallas kernels: none -> 86.2 us  [per_device(): pl.pallas_call(functools.partial(kernel, groups, members), out_shape=(jax...]
    add x4 -> x0, other arithmetic: 42.1 us -> none  [the longest x2 29.5 us: laplacian(): second_diff(padded, 1) + second_diff(padded, 2) + second_diff(padded, 3)]
    slice x2 -> x0, local copies, waits for them, and re-layouts: 14.4 us -> none  [pad_periodic(): after = lax.slice_in_dim(field, 0, 2, axis=dimension)]
    dot_general x2 -> x0, matrix products: 14.3 us -> none  [the longest x1 7.73 us: evolution(): jnp.einsum('fg,gzyx->fzyx', mix_matrix, centre, precision=lax.Precision.H...]
    all_to_all x1 -> x0, starting transfers between devices: 6.88 us -> none  [per_device(): weyl = lax.all_to_all(local, 'dev', split_axis=2, concat_axis=1, tiled=True)]
    div x2 -> x0, other arithmetic: 6.67 us -> none  [first_diff(): return (values[0] - 8.0 * values[1] + 8.0 * values[3] - values[4]) / 12.0]
    ppermute x2 -> x0, starting transfers between devices: 6.52 us -> none  [the longest x1 3.47 us: with_halo(): lax.ppermute(lax.slice_in_dim(block, 0, width, axis=dim), axis, backward)]
  transfers between devices with their start and end apart: 3 -> 0, of which waited for: 2 -> 0; matrix products, arithmetic and copies ran while one was open for 23% -> 0% of each run, Pallas kernels for 0% -> 0%
where the time goes in v1:
time: 91.7 us; the launch traced here: 90.6 us
  Pallas kernels  86.2 us (94%)
  local copies, waits for them, and re-layouts  3.78 us (4%)
    pallas_call x1, Pallas kernels, per_device(): pl.pallas_call(functools.partial(kernel, groups, members), out_shape=(jax...  86.2 us
    unnamed x6, local copies, waits for them, and re-layouts  3.78 us

profile of v1, /device:TPU:0, one launch (start us, length us, event | category | flops | bytes accessed | tf_op | source)
XLA Modules:
  0.0 90.6 jit_solution(3827300031478816269)
XLA Ops:
  0.6 0.0 copy-start
  0.6 0.7 copy-done
  1.3 0.0 copy-start.1
  1.3 0.7 copy-done.1
  2.0 86.2 %evolve.1 = (f32[24,2,128,128]{3,2,1,0:T(8,128)S(1)}, f32[2,16,16,128]{3,2,1,0:T(8,128)S(1)}) custom-call(f32[24,2,128,128]{3,2,1,0:T(8,128)} %fields_ref.1, f32[24,24]{1,0:T(8,128)S(1)} %copy-done, f32[24,24]{1,0:T(8,128)S(1)} %copy-done.1), custom_call_target="tpu_custom_call" | custom-call | tf_op jit(solution)/shard_map/evolve/pallas_call | solution.py:273
  88.2 1.7 %copy.7 = f32[24,2,128,128]{3,2,1,0:T(8,128)} copy(f32[24,2,128,128]{3,2,1,0:T(8,128)S(1)} %get-tuple-element.4) | data formatting | bytes 6291456
  89.9 0.7 copy.8
Async XLA Ops:
  0.6 0.7 copy-start
  1.3 0.7 copy-start.1

commit v2 on v1

--- a/solution.py
+++ b/solution.py
@@ -7,8 +7,9 @@
 from jax.experimental.pallas import tpu as pltpu
 from jax.sharding import PartitionSpec as P
 
-AHEAD = 12
-LAG = 3
+AHEAD = 24
+LAG = 4
+WEYL_STEPS = 4
 TABLE = ((0, 1, 2), (1, 3, 4), (2, 4, 5))
 PAIRS = ((0, 0), (0, 1), (0, 2), (1, 1), (1, 2), (2, 2))
 
@@ -61,8 +62,8 @@
     groups,
     members,
     fields_ref,
-    mix_ref,
-    lap_ref,
+    mix_hbm,
+    lap_hbm,
     rhs_ref,
     weyl_ref,
     own,
@@ -73,7 +74,10 @@
     wtmp,
     wloc,
     wrecv,
+    mix_ref,
+    lap_ref,
     own_sem,
+    mat_sem,
     send_p,
     recv_p,
     send_r,
@@ -97,6 +101,12 @@
 
     load = pltpu.make_async_copy(fields_ref, own, own_sem)
     load.start()
+    small = (
+        pltpu.make_async_copy(mix_hbm, mix_ref, mat_sem.at[0]),
+        pltpu.make_async_copy(lap_hbm, lap_ref, mat_sem.at[1]),
+    )
+    for copy in small:
+        copy.start()
 
     def peer(offset):
         return lax.rem(dev + offset, members)
@@ -114,8 +124,8 @@
 
     def exchange(i, slot):
         return pltpu.make_async_remote_copy(
-            src_ref=fields_ref.at[i],
-            dst_ref=halo.at[slot, i],
+            src_ref=fields_ref.at[i // depth, lax.rem(i, depth)],
+            dst_ref=halo.at[slot, i // depth, lax.rem(i, depth)],
             send_sem=send_p.at[i],
             recv_sem=recv_p.at[i],
             device_id=place(partner),
@@ -124,8 +134,8 @@
 
     def relay(i, slot):
         return pltpu.make_async_remote_copy(
-            src_ref=halo.at[1 - side, i],
-            dst_ref=halo.at[slot, i],
+            src_ref=halo.at[1 - side, i // depth, lax.rem(i, depth)],
+            dst_ref=halo.at[slot, i // depth, lax.rem(i, depth)],
             send_sem=send_r.at[i],
             recv_sem=recv_r.at[i],
             device_id=place(follow),
@@ -142,7 +152,8 @@
             device_id_type=pl.DeviceIdType.MESH,
         )
 
-    ahead = min(AHEAD, count)
+    chunks = count * depth
+    ahead = min(AHEAD, chunks)
 
     @pl.loop(0, ahead)
     def _(i):
@@ -150,24 +161,28 @@
 
     rhs_ref[...] = jnp.zeros_like(rhs_ref)
     load.wait()
+    for copy in small:
+        copy.wait()
 
     def advance(i):
         exchange(i, 1 - side).wait_recv()
         relay(i, side).start()
 
-        @pl.when(i + ahead < count)
+        @pl.when(i + ahead < chunks)
         def _():
             exchange(i + ahead, side).start()
 
-    @pl.loop(0, LAG)
+    @pl.loop(0, LAG * depth)
     def _(i):
         advance(i)
 
-    def weyl_local():
+    def weyl_local(part):
         tiles = rows // 8
-
-        @pl.loop(0, depth * tiles)
-        def _(t):
+        share = depth * tiles // WEYL_STEPS
+
+        @pl.loop(0, share)
+        def _(u):
+            t = part * share + u
             p = t // tiles
             start = pl.multiple_of(lax.rem(t, tiles) * 8, 8)
             strip = pl.ds(start, 8)
@@ -183,9 +198,6 @@
             real, imag = weyl_pair(curv, lap, grad, along_x, along_y, along_z)
             wtmp[0, p, strip, :] = real
             wtmp[1, p, strip, :] = imag
-
-        for m in range(members):
-            wloc[m] = wtmp[:, :, m * per : (m + 1) * per, :]
 
     def process(g):
         for p in range(depth):
@@ -230,16 +242,23 @@
     def _(g):
         @pl.when(g + LAG < count)
         def _():
-            advance(g + LAG)
-
-        relay(g, side).wait_recv()
+            for p in range(depth):
+                advance((g + LAG) * depth + p)
+
+        for p in range(depth):
+            relay(g * depth + p, side).wait_recv()
         process(g)
 
-        @pl.when(g == 11)
-        def _():
-            weyl_local()
-
-        @pl.when(g == 13)
+        @pl.when(jnp.logical_and(g >= 11, g < 11 + WEYL_STEPS))
+        def _():
+            weyl_local(g - 11)
+
+        @pl.when(g == 11 + WEYL_STEPS)
+        def _():
+            for m in range(members):
+                wloc[m] = wtmp[:, :, m * per : (m + 1) * per, :]
+
+        @pl.when(g == 12 + WEYL_STEPS)
         def _():
             for offset in range(1, members):
                 spread(peer(offset), dev).start()
@@ -257,7 +276,7 @@
     for offset in range(1, members):
         spread(peer(offset), dev).wait_send()
 
-    @pl.loop(0, count)
+    @pl.loop(0, chunks)
     def _(i):
         exchange(i, side).wait_send()
         relay(i, side).wait_send()
@@ -277,9 +296,9 @@
             jax.ShapeDtypeStruct((2, depth * members, per, width), jnp.float32),
         ),
         in_specs=[
-            pl.BlockSpec(memory_space=pl.ANY),
-            pl.BlockSpec(memory_space=pltpu.SMEM),
-            pl.BlockSpec(memory_space=pltpu.SMEM),
+            pl.BlockSpec(memory_space=pltpu.HBM),
+            pl.BlockSpec(memory_space=pltpu.HBM),
+            pl.BlockSpec(memory_space=pltpu.HBM),
         ],
         out_specs=(
             pl.BlockSpec(memory_space=pltpu.VMEM),
@@ -294,11 +313,14 @@
             vmem((2, depth) + plane),
             vmem((members, 2, depth, per, width)),
             vmem((members, 2, depth, per, width)),
+            pltpu.SMEM((count, count), jnp.float32),
+            pltpu.SMEM((count, count), jnp.float32),
             dma,
-            dma((count,)),
-            dma((count,)),
-            dma((count,)),
-            dma((count,)),
+            dma((2,)),
+            dma((count * depth,)),
+            dma((count * depth,)),
+            dma((count * depth,)),
+            dma((count * depth,)),
             dma((members,)),
             dma((members,)),
         ],

time: 91.7 us -> 90.4 us (0.986)
  Pallas kernels: 86.2 us -> 84.8 us
    pallas_call x1, Pallas kernels: 86.2 us -> 84.8 us  [per_device(): pl.pallas_call(functools.partial(kernel, groups, members), out_shape=(jax...]
where the time goes in v2:
time: 90.4 us; the launch traced here: 89.3 us
  Pallas kernels  84.8 us (94%)
  local copies, waits for them, and re-layouts  3.78 us (4%)
    pallas_call x1, Pallas kernels, per_device(): pl.pallas_call(functools.partial(kernel, groups, members), out_shape=(jax...  84.8 us
    unnamed x6, local copies, waits for them, and re-layouts  3.78 us

profile of v2, /device:TPU:0, one launch (start us, length us, event | category | flops | bytes accessed | tf_op | source)
XLA Modules:
  0.0 89.3 jit_solution(14133232500096084524)
XLA Ops:
  0.6 0.0 copy-start
  0.6 0.7 copy-done
  1.3 0.0 copy-start.1
  1.3 0.7 copy-done.1
  2.0 84.8 %evolve.1 = (f32[24,2,128,128]{3,2,1,0:T(8,128)S(1)}, f32[2,16,16,128]{3,2,1,0:T(8,128)S(1)}) custom-call(f32[24,2,128,128]{3,2,1,0:T(8,128)} %fields_ref.1, f32[24,24]{1,0:T(8,128)S(1)} %copy-done, f32[24,24]{1,0:T(8,128)S(1)} %copy-done.1), custom_call_target="tpu_custom_call" | custom-call | tf_op jit(solution)/shard_map/evolve/pallas_call | solution.py:292
  86.9 1.7 %copy.7 = f32[24,2,128,128]{3,2,1,0:T(8,128)} copy(f32[24,2,128,128]{3,2,1,0:T(8,128)S(1)} %get-tuple-element.4) | data formatting | bytes 6291456
  88.6 0.7 copy.8
Async XLA Ops:
  0.6 0.7 copy-start
  1.3 0.7 copy-start.1

commit v3 on v2

--- a/solution.py
+++ b/solution.py
@@ -258,7 +258,7 @@
             for m in range(members):
                 wloc[m] = wtmp[:, :, m * per : (m + 1) * per, :]
 
-        @pl.when(g == 12 + WEYL_STEPS)
+        @pl.when(g == count - LAG)
         def _():
             for offset in range(1, members):
                 spread(peer(offset), dev).start()
@@ -328,7 +328,11 @@
             collective_id=0, has_side_effects=True, vmem_limit_bytes=48 * 1024 * 1024
         ),
         name="evolve",
-    )(fields, mix_matrix, laplace_matrix)
+    )(
+        fields,
+        pltpu.with_memory_space_constraint(mix_matrix, pltpu.HBM),
+        pltpu.with_memory_space_constraint(laplace_matrix, pltpu.HBM),
+    )
 
 
 def solution(mesh):

time: 90.4 us -> 88.7 us (0.981); the launches traced: 89.3 us -> 88.6 us
  local copies, waits for them, and re-layouts: 3.78 us -> 2.37 us
    unnamed x6 -> x2, local copies, waits for them, and re-layouts: 3.78 us -> 2.37 us
where the time goes in v3:
time: 88.7 us; the launch traced here: 88.6 us
  Pallas kernels  85.6 us (97%)
  local copies, waits for them, and re-layouts  2.37 us (3%)
    pallas_call x1, Pallas kernels, per_device(): pl.pallas_call(functools.partial(kernel, groups, members), out_shape=(jax...  85.6 us
    unnamed x2, local copies, waits for them, and re-layouts  2.37 us

profile of v3, /device:TPU:0, one launch (start us, length us, event | category | flops | bytes accessed | tf_op | source)
XLA Modules:
  0.0 88.6 jit_solution(13319044928799459197)
XLA Ops:
  0.6 85.6 %evolve.1 = (f32[24,2,128,128]{3,2,1,0:T(8,128)S(1)}, f32[2,16,16,128]{3,2,1,0:T(8,128)S(1)}) custom-call(f32[24,2,128,128]{3,2,1,0:T(8,128)} %fields_ref.1, f32[24,24]{1,0:T(8,128)} %mix_hbm.1, f32[24,24]{1,0:T(8,128)} %lap_hbm.1), custom_call_target="tpu_custom_call" | custom-call | tf_op jit(solution)/shard_map/evolve/pallas_call | solution.py:292
  86.2 1.7 %copy.7 = f32[24,2,128,128]{3,2,1,0:T(8,128)} copy(f32[24,2,128,128]{3,2,1,0:T(8,128)S(1)} %get-tuple-element.4) | data formatting | bytes 6291456
  87.9 0.7 copy.8
